TPU v7x, 32 devices: a whole 2x2x4 slice. The times are simulated.
32 devices in a mesh: dp: 8 (over z, x), tp: 4 (over y, core).
Axes of the slice: x: 2, y: 2, z: 4, core: 2. Of those that a mesh axis runs over, the one named last changes fastest.
Arguments:
- gradients: bfloat16 [8, 4, 5120, 1280], P('dp', None, 'tp'), may hold values from -6 to 6
- right_factor: float32 [4, 1280, 32], replicated, may hold values from -6 to 6
- weights_before: float32 [4, 5120, 1280], P(None, 'tp', 'dp'), may hold values from -0.15625 to 0.15625
- momentum: float32 [4, 5120, 1280], P(None, 'tp', 'dp'), may hold values from -0.3125 to 0.3125
Outputs:
- new_weights: float32 [4, 5120, 1280], P(None, 'tp', 'dp')
- new_basis: float32 [4, 1280, 32], replicated
- new_momentum: float32 [4, 5120, 1280], P(None, 'tp', 'dp')
All inputs are finite; a program needn't handle non-finite values.
Results may differ from a plain program's by a relative error of at most 0.003.
Values sent between devices are 32-bit elements; how exact they have to be, the bound alone decides.
A program may use at most 64 MiB of HBM per device.

v0:
```python
import jax
import jax.numpy as jnp
from jax import lax
from jax.sharding import PartitionSpec as P

RANK = 32


def on_device(gradients, right_factor, weights_before, momentum):
    own_grads = gradients[0]
    part_left = jnp.einsum(
        "liw,lwr->lir",
        own_grads,
        right_factor.astype(jnp.bfloat16),
        preferred_element_type=jnp.float32,
    )
    left = lax.psum(part_left, "dp")
    part_gram = jnp.einsum("lir,lis->lrs", left, left, precision=lax.Precision.HIGHEST)
    small_left = left.astype(jnp.bfloat16)
    gram = lax.psum(part_gram, "tp")
    part_right = jnp.einsum(
        "liw,lir->lwr", own_grads, small_left, preferred_element_type=jnp.float32
    )
    right = lax.psum(part_right, ("dp", "tp"))
    gram = gram + 0.001 * jnp.mean(jnp.diagonal(gram, axis1=1, axis2=2), axis=1)[
        :, None, None
    ] * jnp.eye(RANK, dtype=jnp.float32)
    place = lax.axis_index("dp") * weights_before.shape[2]
    own_right = lax.dynamic_slice_in_dim(right, place, weights_before.shape[2], axis=1)
    root = jnp.linalg.cholesky(gram)
    half = lax.linalg.triangular_solve(
        root, jnp.swapaxes(own_right, 1, 2), left_side=True, lower=True
    )
    mixed = lax.linalg.triangular_solve(root, half, left_side=True, lower=True, transpose_a=True)
    change = jnp.einsum(
        "lir,lrw->liw", left, mixed, precision=lax.Precision.HIGHEST
    ) / lax.axis_size("dp")
    new_momentum = 0.8 * momentum + change
    new_weights = weights_before - 0.05 * new_momentum
    new_basis = right * lax.rsqrt(jnp.mean(right * right, axis=(1, 2), keepdims=True) + 1e-12)
    return (new_weights, new_basis, new_momentum)


def solution(mesh):
    return jax.shard_map(
        on_device,
        mesh=mesh,
        in_specs=(P("dp", None, "tp", None), P(), P(None, "tp", "dp"), P(None, "tp", "dp")),
        out_specs=(P(None, "tp", "dp"), P(), P(None, "tp", "dp")),
        check_vma=False,
    )
```

profile of v0, /device:TPU:0, one launch (start us, length us, event | category | flops | bytes accessed | tf_op | source)
XLA Modules:
  0.0 276.0 jit_solution(18249295536158250338)
XLA Ops:
  7.2 0.0 all-reduce.3.cloned.1.call-start
  7.2 9.6 %fusion.2 = f32[4,1280,32]{1,2,0:T(8,128)} fusion(bf16[1,4,1280,1280]{3,2,1,0:T(8,128)(2,1)} %param.4, f32[4,1280,32]{1,2,0:T(8,128)} %param.5), kind=kOutput, calls=%fused_computation.3 | convolution fusion | flops 419594240 | bytes 14417920 | tf_op jit(solution)/shard_map/liw,lwr->lir/dot_general | solution.py:11
  16.8 0.0 all-reduce.3.cloned.1.call-update
  16.8 0.0 all-reduce.5.cloned.1.call-start
  16.9 0.1 copy.13
  17.0 76.5 %all-reduce.3.cloned.1.call-done = f32[4,1280,32]{1,2,0:T(8,128)} async-done(((f32[4,1280,32]{1,2,0:T(8,128)}), f32[4,1280,32]{1,2,0:T(8,128)}) %all-reduce.3.cloned.1.call-update) | async-done | bytes 655376 | tf_op jit(solution)/shard_map/psum | solution.py:17
  93.4 2.0 fusion.18
  95.5 10.7 %psum.22 = f32[4,32,32]{1,2,0:T(8,128)S(1)} all-reduce(f32[4,32,32]{1,2,0:T(8,128)S(1)} %fusion.18), channel_id=1, replica_groups=mesh['dp'=8,'tp'=4] {'tp'}, use_global_device_ids=true, to_apply=%region_1.0 | all-reduce | flops 4096 | bytes 32768 | tf_op jit(solution)/shard_map/psum | solution.py:20
  106.1 0.5 copy.12
  106.7 0.7 gather_fusion
  107.4 0.1 multiply_add_fusion
  107.5 0.1 copy.14
  107.6 0.1 fusion.15
  107.7 11.7 %custom-call.9 = f32[4,32,32]{2,1,0:T(8,128)S(1)} custom-call(f32[4,32,32]{2,1,0:T(8,128)S(1)} %fusion.15), custom_call_target="Cholesky" | custom-call | tf_op jit(solution)/shard_map/jit(cholesky)/cholesky | solution.py:30
  119.4 8.1 %fusion.5 = f32[4,1280,32]{1,2,0:T(8,128)} fusion(bf16[1,4,1280,1280]{3,2,1,0:T(8,128)(2,1)} %param.4, f32[4,1280,32]{1,2,0:T(8,128)} %all-reduce.3.cloned.1.call-done), kind=kOutput, calls=%fused_computation.8 | convolution fusion | flops 419594240 | bytes 14417920 | tf_op jit(solution)/shard_map/liw,lir->lwr/dot_general | solution.py:21
  127.5 0.0 copy-start
  127.5 0.0 all-reduce.5.cloned.1.call-update
  127.5 0.1 compare_reduce_fusion
  127.7 0.1 select_bitcast_fusion
  127.7 9.8 %custom-call.10 = f32[4,1,32,32]{2,3,1,0:T(8,128)S(1)} custom-call(f32[4,1,32,32]{3,2,1,0:T(8,128)S(1)} %select_bitcast_fusion), custom_call_target="InvertDiagBlocksLowerTriangular" | custom-call | tf_op jit(solution)/shard_map/triangular_solve | solution.py:34
  137.6 119.6 %all-reduce.5.cloned.1.call-done = f32[4,1280,32]{1,2,0:T(8,128)} async-done(((f32[4,1280,32]{1,2,0:T(8,128)}), f32[4,1280,32]{1,2,0:T(8,128)}) %all-reduce.5.cloned.1.call-update) | async-done | bytes 655376 | tf_op jit(solution)/shard_map/psum | solution.py:24
  257.2 1.2 multiply_reduce_fusion
  258.4 1.3 fusion.10
  259.7 0.3 fusion.12
  260.0 2.0 broadcast_multiply_fusion
  262.0 0.0 copy-done
  262.0 7.2 %multiply_subtract_fusion = (f32[4,1280,160]{1,2,0:T(8,128)}, f32[4,1280,160]{1,2,0:T(8,128)}) fusion(f32[4,1280,160]{1,2,0:T(8,128)} %param.6, f32[4,1280,32]{1,2,0:T(8,128)S(1)} %copy-done, f32[4,32,160]{2,1,0:T(8,128)S(1)} %fusion.12, f32[4,1280,160]{1,2,0:T(8,128)} %param.7), kind=kOutput, calls=%fused_computation.7 | convolution fusion | flops 318668800 | bytes 13844480 | tf_op jit(solution)/shard_map/lir,lrw->liw/dot_general | solution.py:35
  (8 shorter events, 0.1 us)
Async XLA Ops:
  7.2 86.3 %all-reduce.3.cloned.1.call-start = ((), (), s32[]{:S(2)}) async-start(), calls=%async_computation | async-start | bytes 1310720 | tf_op jit(solution)/shard_map/psum | solution.py:17
  16.8 240.4 %all-reduce.5.cloned.1.call-start = ((), (), s32[]{:S(2)}) async-start(), calls=%async_computation.1 | async-start | bytes 1310720 | tf_op jit(solution)/shard_map/psum | solution.py:24
  127.5 134.5 %copy-start = (f32[4,1280,32]{1,2,0:T(8,128)S(1)}, f32[4,1280,32]{1,2,0:T(8,128)}, u32[]{:S(2)}) copy-start(f32[4,1280,32]{1,2,0:T(8,128)} %all-reduce.3.cloned.1.call-done) | copy-start | bytes 1966084
Sparse Core Ops, SparseCore 0:
  16.9 76.4 all-reduce.2
  127.6 129.4 all-reduce.4
where the time goes:
time: 276 us
  waiting for transfers between devices  196 us (71%)
  matrix products  28.4 us (10%)
  other arithmetic  25.3 us (9%)
  between operations  14.1 us (5%)
  blocking collectives  10.7 us (4%)
    psum x1, waiting for transfers between devices, on_device(): right = lax.psum(part_right, ('dp', 'tp'))  120 us
    psum x1, waiting for transfers between devices, on_device(): left = lax.psum(part_left, 'dp')  76.5 us
    another operation x4, other arithmetic, on_device(): root = jnp.linalg.cholesky(gram)  11.9 us
    psum x1, blocking collectives, on_device(): gram = lax.psum(part_gram, 'tp')  10.7 us
    another operation x3, other arithmetic, on_device(): lax.linalg.triangular_solve(root, half, left_side=True, lower=True, trans...  9.93 us
    dot_general x1, matrix products, on_device(): jnp.einsum('liw,lwr->lir', own_grads, right_factor.astype(jnp.bfloat16),...  9.56 us
    dot_general x1, matrix products, on_device(): jnp.einsum('liw,lir->lwr', own_grads, small_left, preferred_element_type=...  8.11 us
    dot_general x1, matrix products, on_device(): jnp.einsum('lir,lrw->liw', left, mixed, precision=lax.Precision.HIGHEST)  7.16 us
  transfers between devices with their start and end apart: 2, of which 2 were waited for; matrix products, arithmetic and copies ran while one was open for 4% of the time, Pallas kernels for 0%

commit v1 on v0

--- a/solution.py
+++ b/solution.py
@@ -14,7 +14,9 @@
         right_factor.astype(jnp.bfloat16),
         preferred_element_type=jnp.float32,
     )
-    left = lax.psum(part_left, "dp")
+    left = part_left
+    for hop in (1, 2, 4):
+        left = left + lax.ppermute(left, "dp", [(dev, dev ^ hop) for dev in range(8)])
     part_gram = jnp.einsum("lir,lis->lrs", left, left, precision=lax.Precision.HIGHEST)
     small_left = left.astype(jnp.bfloat16)
     gram = lax.psum(part_gram, "tp")

time: 276 us -> 261 us (0.946)
  waiting for transfers between devices: 196 us -> 177 us
  starting transfers between devices: 0.08 us -> 7.54 us
    psum x1 -> x0, waiting for transfers between devices: 76.5 us -> none  [on_device(): left = lax.psum(part_left, 'dp')]
    ppermute x0 -> x3, waiting for transfers between devices: none -> 56.1 us  [on_device(): lax.ppermute(left, 'dp', [(dev, dev ^ hop) for dev in range(8)])]
    ppermute x0 -> x3, starting transfers between devices: none -> 7.51 us  [on_device(): lax.ppermute(left, 'dp', [(dev, dev ^ hop) for dev in range(8)])]
  transfers between devices with their start and end apart: 2 -> 4, of which waited for: 2 -> 4; matrix products, arithmetic and copies ran while one was open for 4% -> 4% of each run, Pallas kernels for 0% -> 0%
where the time goes in v1:
time: 261 us
  waiting for transfers between devices  177 us (68%)
  matrix products  26 us (10%)
  other arithmetic  24.4 us (9%)
  between operations  14.1 us (5%)
  blocking collectives  10.7 us (4%)
  starting transfers between devices  7.54 us (3%)
    psum x1, waiting for transfers between devices, on_device(): right = lax.psum(part_right, ('dp', 'tp'))  121 us
    ppermute x3, waiting for transfers between devices, on_device(): lax.ppermute(left, 'dp', [(dev, dev ^ hop) for dev in range(8)])  56.1 us
    another operation x4, other arithmetic, on_device(): root = jnp.linalg.cholesky(gram)  11.9 us
    psum x1, blocking collectives, on_device(): gram = lax.psum(part_gram, 'tp')  10.7 us
    another operation x3, other arithmetic, on_device(): lax.linalg.triangular_solve(root, half, left_side=True, lower=True, trans...  9.93 us
    dot_general x1, matrix products, on_device(): jnp.einsum('liw,lwr->lir', own_grads, right_factor.astype(jnp.bfloat16),...  8.69 us
    dot_general x1, matrix products, on_device(): jnp.einsum('liw,lir->lwr', own_grads, small_left, preferred_element_type=...  7.88 us
    ppermute x3, starting transfers between devices, on_device(): lax.ppermute(left, 'dp', [(dev, dev ^ hop) for dev in range(8)])  7.51 us
  transfers between devices with their start and end apart: 4, of which 4 were waited for; matrix products, arithmetic and copies ran while one was open for 4% of the time, Pallas kernels for 0%

profile of v1, /device:TPU:0, one launch (start us, length us, event | category | flops | bytes accessed | tf_op | source)
XLA Modules:
  0.0 261.2 jit_solution(13702040792497572471)
XLA Ops:
  7.2 0.0 all-reduce.2.cloned.1.call-start
  7.2 8.7 %fusion.2 = f32[4,1280,32]{1,2,0:T(8,128)S(1)} fusion(bf16[1,4,1280,1280]{3,2,1,0:T(8,128)(2,1)} %param.4, f32[4,1280,32]{1,2,0:T(8,128)} %param.5), kind=kOutput, calls=%fused_computation.3 | convolution fusion | flops 419594240 | bytes 14417920 | tf_op jit(solution)/shard_map/liw,lwr->lir/dot_general | solution.py:11
  15.9 3.0 %collective-permute-start = (f32[4,1280,32]{1,2,0:T(8,128)S(1)}, f32[4,1280,32]{1,2,0:T(8,128)S(1)}, u32[]{:S(2)}, u32[]{:S(2)}) collective-permute-start(f32[4,1280,32]{1,2,0:T(8,128)S(1)} %fusion.2), channel_id=1, source_target_pairs={{0,4},{4,0},{8,12},{12,8},{16,20},{20,16},{24,28},{28,24},{1,5},{5... | collective-permute-start | bytes 1966088 | tf_op jit(solution)/shard_map/ppermute | solution.py:19
  18.9 14.7 %collective-permute-done = f32[4,1280,32]{1,2,0:T(8,128)S(1)} collective-permute-done((f32[4,1280,32]{1,2,0:T(8,128)S(1)}, f32[4,1280,32]{1,2,0:T(8,128)S(1)}, u32[]{:S(2)}, u32[]{:S(2)}) %collective-permute-start) | collective-permute-done | bytes 655392 | tf_op jit(solution)/shard_map/ppermute | solution.py:19
  33.6 0.1 add.47
  33.7 1.9 collective-permute-start.1
  35.6 14.1 %collective-permute-done.1 = f32[4,1280,32]{1,2,0:T(8,128)S(1)} collective-permute-done((f32[4,1280,32]{1,2,0:T(8,128)S(1)}, f32[4,1280,32]{1,2,0:T(8,128)S(1)}, u32[]{:S(2)}, u32[]{:S(2)}) %collective-permute-start.1) | collective-permute-done | bytes 655392 | tf_op jit(solution)/shard_map/ppermute | solution.py:19
  49.7 0.1 add.48
  49.7 2.6 %collective-permute-start.2 = (f32[4,1280,32]{1,2,0:T(8,128)S(1)}, f32[4,1280,32]{1,2,0:T(8,128)S(1)}, u32[]{:S(2)}, u32[]{:S(2)}) collective-permute-start(f32[4,1280,32]{1,2,0:T(8,128)S(1)} %add.48), channel_id=1, source_target_pairs={{0,16},{4,20},{8,24},{12,28},{16,0},{20,4},{24,8},{28,12},{1,17},{... | collective-permute-start | bytes 1966088 | tf_op jit(solution)/shard_map/ppermute | solution.py:19
  52.4 0.1 copy.13
  52.5 27.3 %collective-permute-done.2 = f32[4,1280,32]{1,2,0:T(8,128)S(1)} collective-permute-done((f32[4,1280,32]{1,2,0:T(8,128)S(1)}, f32[4,1280,32]{1,2,0:T(8,128)S(1)}, u32[]{:S(2)}, u32[]{:S(2)}) %collective-permute-start.2) | collective-permute-done | bytes 655392 | tf_op jit(solution)/shard_map/ppermute | solution.py:19
  79.8 0.1 add.49
  79.9 0.7 fusion.18
  80.5 7.9 %fusion.5 = f32[4,1280,32]{1,2,0:T(8,128)} fusion(bf16[1,4,1280,1280]{3,2,1,0:T(8,128)(2,1)} %param.4, f32[4,1280,32]{1,2,0:T(8,128)S(1)} %add.49), kind=kOutput, calls=%fused_computation.8 | convolution fusion | flops 419594240 | bytes 14417920 | tf_op jit(solution)/shard_map/liw,lir->lwr/dot_general | solution.py:23
  88.4 10.7 %psum.14 = f32[4,32,32]{1,2,0:T(8,128)S(1)} all-reduce(f32[4,32,32]{1,2,0:T(8,128)S(1)} %fusion.18), channel_id=1, replica_groups=mesh['dp'=8,'tp'=4] {'tp'}, use_global_device_ids=true, to_apply=%region_0.0 | all-reduce | flops 4096 | bytes 32768 | tf_op jit(solution)/shard_map/psum | solution.py:22
  99.1 0.5 copy.12
  99.6 0.7 gather_fusion
  100.4 0.1 multiply_add_fusion
  100.4 0.1 copy.14
  100.5 0.1 fusion.15
  100.6 11.7 %custom-call.9 = f32[4,32,32]{2,1,0:T(8,128)S(1)} custom-call(f32[4,32,32]{2,1,0:T(8,128)S(1)} %fusion.15), custom_call_target="Cholesky" | custom-call | tf_op jit(solution)/shard_map/jit(cholesky)/cholesky | solution.py:32
  112.4 0.0 all-reduce.2.cloned.1.call-update
  112.4 0.1 compare_reduce_fusion
  112.5 0.1 select_bitcast_fusion
  112.6 9.8 %custom-call.10 = f32[4,1,32,32]{2,3,1,0:T(8,128)S(1)} custom-call(f32[4,1,32,32]{3,2,1,0:T(8,128)S(1)} %select_bitcast_fusion), custom_call_target="InvertDiagBlocksLowerTriangular" | custom-call | tf_op jit(solution)/shard_map/triangular_solve | solution.py:36
  122.5 120.9 %all-reduce.2.cloned.1.call-done = f32[4,1280,32]{1,2,0:T(8,128)} async-done(((f32[4,1280,32]{1,2,0:T(8,128)}), f32[4,1280,32]{1,2,0:T(8,128)}) %all-reduce.2.cloned.1.call-update) | async-done | bytes 655376 | tf_op jit(solution)/shard_map/psum | solution.py:26
  243.4 1.2 multiply_reduce_fusion
  244.6 1.3 fusion.10
  245.9 0.3 fusion.12
  246.2 0.0 copy-start
  246.2 7.2 %multiply_subtract_fusion = (f32[4,1280,160]{1,2,0:T(8,128)}, f32[4,1280,160]{1,2,0:T(8,128)}) fusion(f32[4,1280,160]{1,2,0:T(8,128)} %param.6, f32[4,1280,32]{1,2,0:T(8,128)S(1)} %add.49, f32[4,32,160]{2,1,0:T(8,128)S(1)} %fusion.12, f32[4,1280,160]{1,2,0:T(8,128)} %param.7), kind=kOutput, calls=%fused_computation.7 | convolution fusion | flops 318668800 | bytes 13844480 | tf_op jit(solution)/shard_map/lir,lrw->liw/dot_general | solution.py:37
  253.4 0.9 broadcast_multiply_fusion
  (9 shorter events, 0.1 us)
Async XLA Ops:
  7.2 236.2 %all-reduce.2.cloned.1.call-start = ((), (), s32[]{:S(2)}) async-start(), calls=%async_computation | async-start | bytes 1310720 | tf_op jit(solution)/shard_map/psum | solution.py:26
  15.9 17.7 %collective-permute-start = (f32[4,1280,32]{1,2,0:T(8,128)S(1)}, f32[4,1280,32]{1,2,0:T(8,128)S(1)}, u32[]{:S(2)}, u32[]{:S(2)}) collective-permute-start(f32[4,1280,32]{1,2,0:T(8,128)S(1)} %fusion.2), channel_id=1, source_target_pairs={{0,4},{4,0},{8,12},{12,8},{16,20},{20,16},{24,28},{28,24},{1,5},{5... | collective-permute-start | bytes 1966088 | tf_op jit(solution)/shard_map/ppermute | solution.py:19
  33.7 16.0 %collective-permute-start.1 = (f32[4,1280,32]{1,2,0:T(8,128)S(1)}, f32[4,1280,32]{1,2,0:T(8,128)S(1)}, u32[]{:S(2)}, u32[]{:S(2)}) collective-permute-start(f32[4,1280,32]{1,2,0:T(8,128)S(1)} %add.47), channel_id=1, source_target_pairs={{0,8},{4,12},{8,0},{12,4},{16,24},{20,28},{24,16},{28,20},{1,9},{5... | collective-permute-start | bytes 1966088 | tf_op jit(solution)/shard_map/ppermute | solution.py:19
  49.7 30.0 %collective-permute-start.2 = (f32[4,1280,32]{1,2,0:T(8,128)S(1)}, f32[4,1280,32]{1,2,0:T(8,128)S(1)}, u32[]{:S(2)}, u32[]{:S(2)}) collective-permute-start(f32[4,1280,32]{1,2,0:T(8,128)S(1)} %add.48), channel_id=1, source_target_pairs={{0,16},{4,20},{8,24},{12,28},{16,0},{20,4},{24,8},{28,12},{1,17},{... | collective-permute-start | bytes 1966088 | tf_op jit(solution)/shard_map/ppermute | solution.py:19
  246.2 7.2 %copy-start = (f32[4,1280,32]{1,2,0:T(8,128)S(1)}, f32[4,1280,32]{1,2,0:T(8,128)}, u32[]{:S(2)}) copy-start(f32[4,1280,32]{1,2,0:T(8,128)} %all-reduce.2.cloned.1.call-done) | copy-start | bytes 1966084
Sparse Core Ops, SparseCore 0:
  112.5 130.8 all-reduce.1
